TPU v7x, 512 devices: a whole 4x4x16 slice. The times are simulated.
512 devices in a mesh: row: 16 (over z), col: 16 (over y, x), layer: 2 (over core).
Axes of the slice: x: 4, y: 4, z: 16, core: 2. Of those that a mesh axis runs over, the one named last changes fastest.
Arguments:
- ratings: bfloat16 [32768, 16384], P('row', ('col', 'layer')), may hold values from -6 to 6
- tile_mask: int32 [256, 128], P('row', ('col', 'layer')), may hold values 0 or 1
- tile_counts: int32 [256, 128], P('row', ('col', 'layer')), may hold values from 1 to 16384
- user_factor: float32 [256, 32768], P(('col', 'layer'), 'row'), may hold values from -1.5 to 1.5
- item_factor: float32 [256, 16384], P('row', ('col', 'layer')), may hold values from -1.5 to 1.5
Outputs:
- new_user: float32 [256, 32768], P(('col', 'layer'), 'row')
- new_item: float32 [256, 16384], P('row', ('col', 'layer'))
- loss_value: float32 [], replicated
- grad_norm: float32 [], replicated
All inputs are finite; a program needn't handle non-finite values. No bound on the sum of `tile_mask` on one device may be relied on, other than what follows from the above.
Results may differ from a plain program's by a relative error of at most 0.0049.
Values may be sent and summed in bfloat16 or wider, within the bound.
No kernel may reach another device: no remote copies, remote signals or barrier semaphores. Data moves between devices by JAX's collectives and lax.ppermute only.
A program may use at most 64 MiB of HBM per device.

v0:
```python
import jax
import jax.numpy as jnp
from jax import lax
from jax.sharding import Mesh
from jax.sharding import PartitionSpec as P

TILE = 128
COL_LAYER = ("col_0", "col_1", "layer")
ROW_COL_LAYER = ("row", "col_0", "col_1", "layer")
epsilon = 1e-12
trust_ratio = 0.2


def from_everyone(array, axis):
    count = lax.axis_size(axis)
    return lax.all_to_all(
        jnp.broadcast_to(array[None], (count, *array.shape)), axis, 0, 0, tiled=True
    )


def joined_along(blocks, dim):
    dims = list(blocks.shape[1:])
    dims[dim] *= blocks.shape[0]
    return jnp.moveaxis(blocks, 0, dim).reshape(dims)


def gather_directly(array, axis, dim):
    blocks = from_everyone(array, axis)
    return joined_along(blocks, dim)


def by_axis(array, axes):
    for axis in axes:
        array = lax.psum(array, axis)
    return array


def in_blocks(array, dim, count):
    dims = array.shape
    blocks = array.reshape(*dims[:dim], count, dims[dim] // count, *dims[dim + 1 :])
    return jnp.moveaxis(blocks, dim, 0)


def sent_and_summed(array, axis, dim):
    blocks = in_blocks(array, dim, lax.axis_size(axis))
    arrived = lax.all_to_all(blocks, axis, split_axis=0, concat_axis=0, tiled=True)
    return arrived.astype(jnp.float32).sum(axis=0)


def tile_weights(mask_rows, count_rows):
    side = TILE
    position = lax.broadcasted_iota(jnp.int32, (side, side), 0) * side + lax.broadcasted_iota(
        jnp.int32, (side, side), 1
    )
    observed = (mask_rows[:, None, :, None] == 1) & (
        position[None, :, None, :] < count_rows[:, None, :, None]
    )
    return observed.astype(jnp.float32).reshape(
        mask_rows.shape[0] * side, mask_rows.shape[1] * side
    )


def body(ratings, tile_mask, tile_counts, user_factor, item_factor):
    user_low = user_factor.astype(jnp.bfloat16)
    item_low = item_factor.astype(jnp.bfloat16)
    user_rows = gather_directly(user_low, COL_LAYER, 0)
    item_cols = gather_directly(item_low, "row", 0)
    count_local = jnp.sum(tile_mask * tile_counts).astype(jnp.float32)
    factor_local = jnp.sum(user_factor * user_factor) + jnp.sum(item_factor * item_factor)
    predicted = lax.dot_general(
        user_rows, item_cols, (((0,), (0,)), ((), ())), preferred_element_type=jnp.float32
    )
    residual = tile_weights(tile_mask, tile_counts) * (predicted - ratings.astype(jnp.float32))
    scaled = residual.astype(jnp.bfloat16)
    error_local = jnp.sum(residual * residual)
    count_sum, factor_sum, error_sum = (
        by_axis(count_local, ROW_COL_LAYER),
        by_axis(factor_local, ROW_COL_LAYER),
        by_axis(error_local, ROW_COL_LAYER),
    )
    factor_part = user_rows
    raw_item = sent_and_summed(
        jnp.dot(factor_part, scaled, preferred_element_type=jnp.float32).astype(jnp.bfloat16),
        "row",
        0,
    )
    factor_part = item_cols
    raw_user = sent_and_summed(
        lax.dot_general(
            factor_part, scaled, (((1,), (1,)), ((), ())), preferred_element_type=jnp.float32
        ).astype(jnp.bfloat16),
        COL_LAYER,
        0,
    )
    gradient_local = jnp.sum(raw_user * raw_user) + jnp.sum(raw_item * raw_item)
    gradient_sum = by_axis(gradient_local, ROW_COL_LAYER)
    observed_total = jnp.maximum(count_sum, jnp.float32(1.0))
    loss_value = error_sum / observed_total
    grad_norm = 2.0 / observed_total * jnp.sqrt(gradient_sum + epsilon)
    factor_norm = jnp.sqrt(factor_sum + epsilon)
    rate = trust_ratio * factor_norm / grad_norm
    step_size = rate * (2.0 / observed_total)
    new_user = user_factor - step_size * raw_user
    new_item = item_factor - step_size * raw_item
    return (new_user, new_item, loss_value, grad_norm)


def solution(mesh):
    finer = Mesh(
        mesh.devices.reshape(mesh.shape["row"], 4, 4, mesh.shape["layer"]),
        ("row", "col_0", "col_1", "layer"),
    )
    return jax.shard_map(
        body,
        mesh=finer,
        in_specs=(
            P("row", COL_LAYER),
            P("row", COL_LAYER),
            P("row", COL_LAYER),
            P(COL_LAYER, "row"),
            P("row", COL_LAYER),
        ),
        out_specs=(P(COL_LAYER, "row"), P("row", COL_LAYER), P(), P()),
        check_vma=False,
    )
```

profile of v0, /device:TPU:1, one launch (start us, length us, event | category | flops | bytes accessed | tf_op | source)
XLA Modules:
  0.0 176.2 jit_solution(6132000480755298234)
XLA Ops:
  0.6 0.0 copy-start.3
  0.6 0.0 copy-start.2
  0.7 1.4 multiply_reduce_fusion.4
  2.1 0.7 broadcast_in_dim.5
  2.8 15.7 %all-to-all-start.1 = ((bf16[16,16,512]{2,1,0:T(8,128)(2,1)}), bf16[16,16,512]{2,1,0:T(8,128)(2,1)S(1)}, u32[]{:S(2)}, u32[]{:S(2)}) async-start(bf16[16,16,512]{2,1,0:T(8,128)(2,1)} %broadcast_in_dim.5), calls=%async_computation.1 | async-start | bytes 524288 | tf_op jit(solution)/shard_map/all_to_all | solution.py:16
  18.6 1.5 multiply_reduce_fusion.2
  20.1 12.2 %all-to-all-done.1 = bf16[16,16,512]{2,1,0:T(8,128)(2,1)S(1)} async-done(((bf16[16,16,512]{2,1,0:T(8,128)(2,1)}), bf16[16,16,512]{2,1,0:T(8,128)(2,1)S(1)}, u32[]{:S(2)}, u32[]{:S(2)}) %all-to-all-start.1) | async-done | bytes 262176 | tf_op jit(solution)/shard_map/all_to_all | solution.py:16
  32.3 1.1 broadcast_in_dim.4
  33.4 12.6 %all-to-all-start = ((bf16[32,8,2048]{2,1,0:T(8,128)(2,1)}), bf16[32,8,2048]{2,1,0:T(8,128)(2,1)S(1)}, u32[]{:S(2)}, u32[]{:S(2)}) async-start(bf16[32,8,2048]{2,1,0:T(8,128)(2,1)} %broadcast_in_dim.4), calls=%async_computation | async-start | bytes 2097152 | tf_op jit(solution)/shard_map/all_to_all | solution.py:16
  46.1 0.1 copy.9
  46.2 0.1 copy.10
  46.3 0.1 iota_add_fusion
  46.4 1.4 compare_and_fusion
  47.9 15.3 %all-to-all-done = bf16[32,8,2048]{2,1,0:T(8,128)(2,1)S(1)} async-done(((bf16[32,8,2048]{2,1,0:T(8,128)(2,1)}), bf16[32,8,2048]{2,1,0:T(8,128)(2,1)S(1)}, u32[]{:S(2)}, u32[]{:S(2)}) %all-to-all-start) | async-done | bytes 1048608 | tf_op jit(solution)/shard_map/all_to_all | solution.py:16
  63.1 4.1 %multiply_reduce_fusion = (f32[]{:T(128)}, bf16[2048,512]{1,0:T(8,128)(2,1)S(1)}) fusion(bf16[2048,512]{1,0:T(8,128)(2,1)} %param.5, bf16[256,512]{1,0:T(8,128)(2,1)S(1)} %bitcast.24, bf16[32,8,2048]{2,1,0:T(8,128)(2,1)S(1)} %all-to-all-done, pred[256,8,4,128]{3,2,1,0:T(4,128)(4,1)S(1)} %bitcast.23), kind=kOutput, calls=%fused_computation | convolution fusion | flops 543162368 | bytes 6553604 | tf_op jit(solution)/shard_map/dot_general | solution.py:70
  67.3 1.4 convolution_convert_fusion.1
  68.7 0.0 copy-done.4
  68.7 5.5 %all-to-all-start.3 = ((bf16[16,16,512]{2,1,0:T(8,128)(2,1)}), bf16[16,16,512]{2,1,0:T(8,128)(2,1)S(1)}, u32[]{:S(2)}, u32[]{:S(2)}) async-start(bf16[16,16,512]{2,1,0:T(8,128)(2,1)} %bitcast.5), calls=%async_computation.3 | async-start | bytes 524288 | tf_op jit(solution)/shard_map/all_to_all | solution.py:46
  74.2 3.3 %fusion = bf16[32,8,2048]{2,1,0:T(8,128)(2,1)} fusion(bf16[256,512]{1,0:T(8,128)(2,1)S(1)} %bitcast.25, bf16[2048,512]{1,0:T(8,128)(2,1)} %copy-done.4), kind=kOutput, calls=%fused_computation.4 | convolution fusion | flops 537395200 | bytes 3407872 | tf_op jit(solution)/shard_map/dot_general | solution.py:89
  77.5 10.7 %all-to-all-done.3 = bf16[16,16,512]{2,1,0:T(8,128)(2,1)S(1)} async-done(((bf16[16,16,512]{2,1,0:T(8,128)(2,1)}), bf16[16,16,512]{2,1,0:T(8,128)(2,1)S(1)}, u32[]{:S(2)}, u32[]{:S(2)}) %all-to-all-start.3) | async-done | bytes 262176 | tf_op jit(solution)/shard_map/all_to_all | solution.py:46
  88.2 8.8 %all-to-all-start.2 = ((bf16[32,8,2048]{2,1,0:T(8,128)(2,1)}), bf16[32,8,2048]{2,1,0:T(8,128)(2,1)S(1)}, u32[]{:S(2)}, u32[]{:S(2)}) async-start(bf16[32,8,2048]{2,1,0:T(8,128)(2,1)} %fusion), calls=%async_computation.2 | async-start | bytes 2097152 | tf_op jit(solution)/shard_map/all_to_all | solution.py:46
  97.0 0.6 multiply_reduce_fusion.5
  99.6 0.6 multiply_reduce_fusion.3
  100.2 13.9 %all-to-all-done.2 = bf16[32,8,2048]{2,1,0:T(8,128)(2,1)S(1)} async-done(((bf16[32,8,2048]{2,1,0:T(8,128)(2,1)}), bf16[32,8,2048]{2,1,0:T(8,128)(2,1)S(1)}, u32[]{:S(2)}, u32[]{:S(2)}) %all-to-all-start.2) | async-done | bytes 1048608 | tf_op jit(solution)/shard_map/all_to_all | solution.py:46
  114.1 0.2 convert_reduce_fusion
  114.2 0.6 multiply_reduce_fusion.1
  116.2 24.6 %all-reduce = (f32[]{:T(128)}, f32[]{:T(128)}, f32[]{:T(128)}, f32[]{:T(128)}) all-reduce(f32[]{:T(128)S(6)} %add.51, f32[]{:T(128)S(6)} %convert_element_type.35, f32[]{:T(128)S(6)} %add.54, f32[]{:T(128)} %get-tuple-element.24), channel_id=1, replica_groups=mesh['row'=16,'col_0'=4,'col_1'=4,'layer'=2] {'row'}, use_global_device_ids=true, to_apply=%region_2.0 | all-reduce | flops 4 | bytes 32 | tf_op jit(solution)/shard_map/psum | solution.py:34
  140.8 7.1 %all-reduce.2 = (f32[]{:T(128)}, f32[]{:T(128)}, f32[]{:T(128)}, f32[]{:T(128)}) all-reduce(f32[]{:T(128)} %get-tuple-element.4, f32[]{:T(128)} %get-tuple-element.5, f32[]{:T(128)} %get-tuple-element.6, f32[]{:T(128)} %get-tuple-element.7), channel_id=1, replica_groups=mesh['row'=16,'col_0'=4,'col_1'=4,'layer'=2] {'col_0'}, use_global_device_ids=true, to_apply=%region_3.0 | all-reduce | flops 4 | bytes 32 | tf_op jit(solution)/shard_map/psum | solution.py:34
  147.9 8.6 %all-reduce.1 = (f32[]{:T(128)}, f32[]{:T(128)}, f32[]{:T(128)}, f32[]{:T(128)}) all-reduce(f32[]{:T(128)} %get-tuple-element.12, f32[]{:T(128)} %get-tuple-element.13, f32[]{:T(128)} %get-tuple-element.14, f32[]{:T(128)} %get-tuple-element.15), channel_id=1, replica_groups=mesh['row'=16,'col_0'=4,'col_1'=4,'layer'=2] {'col_1'}, use_global_device_ids=true, to_apply=%region_4.0 | all-reduce | flops 4 | bytes 32 | tf_op jit(solution)/shard_map/psum | solution.py:34
  156.5 13.3 %all-reduce.3 = (f32[]{:T(128)}, f32[]{:T(128)}, f32[]{:T(128)}, f32[]{:T(128)}) all-reduce(f32[]{:T(128)} %get-tuple-element.8, f32[]{:T(128)} %get-tuple-element.9, f32[]{:T(128)} %get-tuple-element.10, f32[]{:T(128)} %get-tuple-element.11), channel_id=1, replica_groups=mesh['row'=16,'col_0'=4,'col_1'=4,'layer'=2] {'layer'}, use_global_device_ids=true, to_apply=%region_5.0 | all-reduce | flops 4 | bytes 32 | tf_op jit(solution)/shard_map/psum | solution.py:34
  171.9 0.6 multiply_subtract_fusion.1
  172.6 0.6 multiply_subtract_fusion
  (10 shorter events, 0.1 us)
Async XLA Ops:
  0.6 45.5 %copy-start.3 = (s32[16,4]{0,1:T(4,128)S(1)}, s32[16,4]{0,1:T(4,128)}, u32[]{:S(2)}) copy-start(s32[16,4]{0,1:T(4,128)} %param.6) | copy-start | bytes 772
  0.6 45.6 %copy-start.2 = (s32[16,4]{0,1:T(4,128)S(1)}, s32[16,4]{0,1:T(4,128)}, u32[]{:S(2)}) copy-start(s32[16,4]{0,1:T(4,128)} %param.7) | copy-start | bytes 772
  2.8 29.5 %all-to-all-start.1 = ((bf16[16,16,512]{2,1,0:T(8,128)(2,1)}), bf16[16,16,512]{2,1,0:T(8,128)(2,1)S(1)}, u32[]{:S(2)}, u32[]{:S(2)}) async-start(bf16[16,16,512]{2,1,0:T(8,128)(2,1)} %broadcast_in_dim.5), calls=%async_computation.1 | async-start | bytes 524288 | tf_op jit(solution)/shard_map/all_to_all | solution.py:16
  33.4 29.7 %all-to-all-start = ((bf16[32,8,2048]{2,1,0:T(8,128)(2,1)}), bf16[32,8,2048]{2,1,0:T(8,128)(2,1)S(1)}, u32[]{:S(2)}, u32[]{:S(2)}) async-start(bf16[32,8,2048]{2,1,0:T(8,128)(2,1)} %broadcast_in_dim.4), calls=%async_computation | async-start | bytes 2097152 | tf_op jit(solution)/shard_map/all_to_all | solution.py:16
  67.3 1.4 copy-start.4
  68.7 19.5 %all-to-all-start.3 = ((bf16[16,16,512]{2,1,0:T(8,128)(2,1)}), bf16[16,16,512]{2,1,0:T(8,128)(2,1)S(1)}, u32[]{:S(2)}, u32[]{:S(2)}) async-start(bf16[16,16,512]{2,1,0:T(8,128)(2,1)} %bitcast.5), calls=%async_computation.3 | async-start | bytes 524288 | tf_op jit(solution)/shard_map/all_to_all | solution.py:46
  77.5 94.4 %copy-start.1 = (f32[16,512]{1,0:T(8,128)S(1)}, f32[16,512]{1,0:T(8,128)}, u32[]{:S(2)}) copy-start(f32[16,512]{1,0:T(8,128)} %param.9) | copy-start | bytes 98308
  77.5 95.0 %copy-start = (f32[8,2048]{1,0:T(8,128)S(1)}, f32[8,2048]{1,0:T(8,128)}, u32[]{:S(2)}) copy-start(f32[8,2048]{1,0:T(8,128)} %param.8) | copy-start | bytes 196612
  88.2 25.9 %all-to-all-start.2 = ((bf16[32,8,2048]{2,1,0:T(8,128)(2,1)}), bf16[32,8,2048]{2,1,0:T(8,128)(2,1)S(1)}, u32[]{:S(2)}, u32[]{:S(2)}) async-start(bf16[32,8,2048]{2,1,0:T(8,128)(2,1)} %fusion), calls=%async_computation.2 | async-start | bytes 2097152 | tf_op jit(solution)/shard_map/all_to_all | solution.py:46
where the time goes:
time: 177 us; the launch traced here: 176 us
  blocking collectives  53.6 us (30%)
  waiting for transfers between devices  52.1 us (29%)
  starting transfers between devices  42.6 us (24%)
  between operations  9.06 us (5%)
  matrix products  8.87 us (5%)
  other arithmetic  7.83 us (4%)
  local copies, waits for them, and re-layouts  2.03 us (1%)
    psum x4, blocking collectives, by_axis(): array = lax.psum(array, axis)  53.6 us
    all_to_all x2, starting transfers between devices, from_everyone(): lax.all_to_all(jnp.broadcast_to(array[None], (count, *array.shape)), axis...  28.4 us
    all_to_all x2, waiting for transfers between devices, from_everyone(): lax.all_to_all(jnp.broadcast_to(array[None], (count, *array.shape)), axis...  27.5 us
    all_to_all x2, waiting for transfers between devices, sent_and_summed(): lax.all_to_all(blocks, axis, split_axis=0, concat_axis=0, tiled=True)  24.6 us
    all_to_all x2, starting transfers between devices, sent_and_summed(): lax.all_to_all(blocks, axis, split_axis=0, concat_axis=0, tiled=True)  14.3 us
    dot_general x1, matrix products, body(): lax.dot_general(user_rows, item_cols, (((0,), (0,)), ((), ())), preferred...  4.12 us
  transfers between devices with their start and end apart: 4, of which 4 were waited for; matrix products, arithmetic and copies ran while one was open for 4% of the time, Pallas kernels for 0%

commit v1 on v0

--- a/solution.py
+++ b/solution.py
@@ -9,6 +9,12 @@
 ROW_COL_LAYER = ("row", "col_0", "col_1", "layer")
 epsilon = 1e-12
 trust_ratio = 0.2
+
+
+def summed_here(x, name):
+    parts = lax.all_gather(x, name, axis=0, tiled=False)
+    total = parts.sum(axis=0)
+    return total
 
 
 def from_everyone(array, axis):
@@ -31,7 +37,7 @@
 
 def by_axis(array, axes):
     for axis in axes:
-        array = lax.psum(array, axis)
+        array = summed_here(array, axis)
     return array
 
 

time: 177 us -> 205 us (1.16)
  local copies, waits for them, and re-layouts: 2.03 us -> 28.5 us
  other arithmetic: 7.83 us -> 17.4 us
  waiting for transfers between devices: 52.1 us -> 45.8 us
  blocking collectives: 53.6 us -> 51 us
    psum x4 -> x0, blocking collectives: 53.6 us -> none  [by_axis(): array = lax.psum(array, axis)]
    unnamed x0 -> x4, blocking collectives: none -> 51 us
    unnamed x11 -> x47, local copies, waits for them, and re-layouts: 0.1 us -> 26.6 us
    reduce_sum x0 -> x16, other arithmetic: none -> 9.61 us  [summed_here(): total = parts.sum(axis=0)]
    all_to_all x2, waiting for transfers between devices: 24.6 us -> 19 us  [sent_and_summed(): lax.all_to_all(blocks, axis, split_axis=0, concat_axis=0, tiled=True)]
  transfers between devices with their start and end apart: 4 -> 4, of which waited for: 4 -> 4; matrix products, arithmetic and copies ran while one was open for 4% -> 7% of each run, Pallas kernels for 0% -> 0%
where the time goes in v1:
time: 205 us; the launch traced here: 203 us
  blocking collectives  51 us (25%)
  waiting for transfers between devices  45.8 us (22%)
  starting transfers between devices  42.6 us (21%)
  local copies, waits for them, and re-layouts  28.5 us (14%)
  other arithmetic  17.4 us (8%)
  between operations  9.08 us (4%)
  matrix products  8.84 us (4%)
    unnamed x4, blocking collectives  51 us
    all_to_all x2, starting transfers between devices, from_everyone(): lax.all_to_all(jnp.broadcast_to(array[None], (count, *array.shape)), axis...  28.4 us
    all_to_all x2, waiting for transfers between devices, from_everyone(): lax.all_to_all(jnp.broadcast_to(array[None], (count, *array.shape)), axis...  26.9 us
    unnamed x47, local copies, waits for them, and re-layouts  26.6 us
    all_to_all x2, waiting for transfers between devices, sent_and_summed(): lax.all_to_all(blocks, axis, split_axis=0, concat_axis=0, tiled=True)  19 us
    all_to_all x2, starting transfers between devices, sent_and_summed(): lax.all_to_all(blocks, axis, split_axis=0, concat_axis=0, tiled=True)  14.3 us
    reduce_sum x16, other arithmetic, summed_here(): total = parts.sum(axis=0)  9.61 us
  transfers between devices with their start and end apart: 4, of which 4 were waited for; matrix products, arithmetic and copies ran while one was open for 7% of the time, Pallas kernels for 0%

profile of v1, /device:TPU:1, one launch (start us, length us, event | category | flops | bytes accessed | tf_op | source)
XLA Modules:
  0.0 203.3 jit_solution(6204629614202432438)
XLA Ops:
  0.6 1.4 multiply_reduce_fusion.4
  2.8 15.7 %all-to-all-start.1 = ((bf16[16,16,512]{2,1,0:T(8,128)(2,1)}), bf16[16,16,512]{2,1,0:T(8,128)(2,1)S(1)}, u32[]{:S(2)}, u32[]{:S(2)}) async-start(bf16[16,16,512]{2,1,0:T(8,128)(2,1)} %broadcast_in_dim.5), calls=%async_computation.1 | async-start | bytes 524288 | tf_op jit(solution)/shard_map/all_to_all | solution.py:22
  19.3 1.5 multiply_reduce_fusion.2
  20.8 11.5 %all-to-all-done.1 = bf16[16,16,512]{2,1,0:T(8,128)(2,1)S(1)} async-done(((bf16[16,16,512]{2,1,0:T(8,128)(2,1)}), bf16[16,16,512]{2,1,0:T(8,128)(2,1)S(1)}, u32[]{:S(2)}, u32[]{:S(2)}) %all-to-all-start.1) | async-done | bytes 262176 | tf_op jit(solution)/shard_map/all_to_all | solution.py:22
  33.4 12.6 %all-to-all-start = ((bf16[32,8,2048]{2,1,0:T(8,128)(2,1)}), bf16[32,8,2048]{2,1,0:T(8,128)(2,1)S(1)}, u32[]{:S(2)}, u32[]{:S(2)}) async-start(bf16[32,8,2048]{2,1,0:T(8,128)(2,1)} %broadcast_in_dim.4), calls=%async_computation | async-start | bytes 2097152 | tf_op jit(solution)/shard_map/all_to_all | solution.py:22
  46.3 1.4 compare_and_fusion
  47.8 15.4 %all-to-all-done = bf16[32,8,2048]{2,1,0:T(8,128)(2,1)S(1)} async-done(((bf16[32,8,2048]{2,1,0:T(8,128)(2,1)}), bf16[32,8,2048]{2,1,0:T(8,128)(2,1)S(1)}, u32[]{:S(2)}, u32[]{:S(2)}) %all-to-all-start) | async-done | bytes 1048608 | tf_op jit(solution)/shard_map/all_to_all | solution.py:22
  63.1 4.1 %multiply_reduce_fusion = (f32[]{:T(128)}, bf16[2048,512]{1,0:T(8,128)(2,1)S(1)}) fusion(bf16[2048,512]{1,0:T(8,128)(2,1)} %param.5, bf16[256,512]{1,0:T(8,128)(2,1)S(1)} %bitcast.44, bf16[32,8,2048]{2,1,0:T(8,128)(2,1)S(1)} %all-to-all-done, pred[256,8,4,128]{3,2,1,0:T(4,128)(4,1)S(1)} %bitcast.43), kind=kOutput, calls=%fused_computation | convolution fusion | flops 543162368 | bytes 6553604 | tf_op jit(solution)/shard_map/dot_general | solution.py:76
  67.2 1.4 convolution_convert_fusion.1
  68.7 5.5 %all-to-all-start.3 = ((bf16[16,16,512]{2,1,0:T(8,128)(2,1)}), bf16[16,16,512]{2,1,0:T(8,128)(2,1)S(1)}, u32[]{:S(2)}, u32[]{:S(2)}) async-start(bf16[16,16,512]{2,1,0:T(8,128)(2,1)} %bitcast.17), calls=%async_computation.3 | async-start | bytes 524288 | tf_op jit(solution)/shard_map/all_to_all | solution.py:52
  74.2 3.3 %fusion = bf16[32,8,2048]{2,1,0:T(8,128)(2,1)} fusion(bf16[256,512]{1,0:T(8,128)(2,1)S(1)} %bitcast.45, bf16[2048,512]{1,0:T(8,128)(2,1)} %copy-done.4), kind=kOutput, calls=%fused_computation.4 | convolution fusion | flops 537395200 | bytes 3407872 | tf_op jit(solution)/shard_map/dot_general | solution.py:95
  77.5 10.7 %all-to-all-done.3 = bf16[16,16,512]{2,1,0:T(8,128)(2,1)S(1)} async-done(((bf16[16,16,512]{2,1,0:T(8,128)(2,1)}), bf16[16,16,512]{2,1,0:T(8,128)(2,1)S(1)}, u32[]{:S(2)}, u32[]{:S(2)}) %all-to-all-start.3) | async-done | bytes 262176 | tf_op jit(solution)/shard_map/all_to_all | solution.py:52
  88.2 8.8 %all-to-all-start.2 = ((bf16[32,8,2048]{2,1,0:T(8,128)(2,1)}), bf16[32,8,2048]{2,1,0:T(8,128)(2,1)S(1)}, u32[]{:S(2)}, u32[]{:S(2)}) async-start(bf16[32,8,2048]{2,1,0:T(8,128)(2,1)} %fusion), calls=%async_computation.2 | async-start | bytes 2097152 | tf_op jit(solution)/shard_map/all_to_all | solution.py:52
  99.5 1.3 dynamic-slice.1
  103.7 1.4 dynamic-update-slice.12
  105.7 8.3 %all-to-all-done.2 = bf16[32,8,2048]{2,1,0:T(8,128)(2,1)S(1)} async-done(((bf16[32,8,2048]{2,1,0:T(8,128)(2,1)}), bf16[32,8,2048]{2,1,0:T(8,128)(2,1)S(1)}, u32[]{:S(2)}, u32[]{:S(2)}) %all-to-all-start.2) | async-done | bytes 1048608 | tf_op jit(solution)/shard_map/all_to_all | solution.py:52
  116.9 23.9 %all-reduce.16 = (f32[16]{0:T(128)S(1)}, f32[16]{0:T(128)S(1)}, f32[16]{0:T(128)S(1)}, f32[16]{0:T(128)S(1)}) all-reduce(f32[16]{0:T(128)S(1)} %dynamic-update-slice, f32[16]{0:T(128)S(1)} %dynamic-update-slice.4, f32[16]{0:T(128)S(1)} %dynamic-update-slice.8, ...), channel_id=1, replica_groups=mesh['row'=16,'col_0'=4,'col_1'=4,'layer'=2] {'row'}, use_global_device_ids=true, to_apply=%add | all-reduce | flops 64 | bytes 512
  142.0 1.4 dynamic-update-slice.13
  143.5 1.4 dynamic-update-slice.9
  145.5 1.4 dynamic-update-slice.5
  147.6 1.4 dynamic-update-slice.1
  150.3 6.5 %all-reduce.18 = (f32[4]{0:T(128)S(1)}, f32[4]{0:T(128)S(1)}, f32[4]{0:T(128)S(1)}, f32[4]{0:T(128)S(1)}) all-reduce(f32[4]{0:T(128)S(1)} %dynamic-update-slice.1, f32[4]{0:T(128)S(1)} %dynamic-update-slice.5, f32[4]{0:T(128)S(1)} %dynamic-update-slice.9, ...), channel_id=1, replica_groups=mesh['row'=16,'col_0'=4,'col_1'=4,'layer'=2] {'col_0'}, use_global_device_ids=true, to_apply=%add.1 | all-reduce | flops 16 | bytes 128
  158.0 1.4 dynamic-update-slice.10
  159.4 1.4 dynamic-update-slice.14
  161.4 1.4 dynamic-update-slice.6
  163.4 1.4 dynamic-update-slice.2
  166.0 7.9 %all-reduce.17 = (f32[4]{0:T(128)S(1)}, f32[4]{0:T(128)S(1)}, f32[4]{0:T(128)S(1)}, f32[4]{0:T(128)S(1)}) all-reduce(f32[4]{0:T(128)S(1)} %dynamic-update-slice.2, f32[4]{0:T(128)S(1)} %dynamic-update-slice.6, f32[4]{0:T(128)S(1)} %dynamic-update-slice.10, ...), channel_id=1, replica_groups=mesh['row'=16,'col_0'=4,'col_1'=4,'layer'=2] {'col_1'}, use_global_device_ids=true, to_apply=%add.2 | all-reduce | flops 16 | bytes 128
  175.2 1.4 dynamic-update-slice.11
  176.6 1.4 dynamic-update-slice.15
  178.6 1.4 dynamic-update-slice.7
  180.6 1.4 dynamic-update-slice.3
  182.0 12.6 %all-reduce.19 = (f32[2]{0:T(128)S(1)}, f32[2]{0:T(128)S(1)}, f32[2]{0:T(128)S(1)}, f32[2]{0:T(128)S(1)}) all-reduce(f32[2]{0:T(128)S(1)} %dynamic-update-slice.3, f32[2]{0:T(128)S(1)} %dynamic-update-slice.7, f32[2]{0:T(128)S(1)} %dynamic-update-slice.11, ...), channel_id=1, replica_groups=mesh['row'=16,'col_0'=4,'col_1'=4,'layer'=2] {'layer'}, use_global_device_ids=true, to_apply=%add.3 | all-reduce | flops 8 | bytes 64
  (62 shorter events, 21.8 us)
Async XLA Ops:
  0.6 45.5 %copy-start.3 = (s32[16,4]{0,1:T(4,128)S(1)}, s32[16,4]{0,1:T(4,128)}, u32[]{:S(2)}) copy-start(s32[16,4]{0,1:T(4,128)} %param.6) | copy-start | bytes 772
  2.8 29.5 %all-to-all-start.1 = ((bf16[16,16,512]{2,1,0:T(8,128)(2,1)}), bf16[16,16,512]{2,1,0:T(8,128)(2,1)S(1)}, u32[]{:S(2)}, u32[]{:S(2)}) async-start(bf16[16,16,512]{2,1,0:T(8,128)(2,1)} %broadcast_in_dim.5), calls=%async_computation.1 | async-start | bytes 524288 | tf_op jit(solution)/shard_map/all_to_all | solution.py:22
  33.4 29.7 %all-to-all-start = ((bf16[32,8,2048]{2,1,0:T(8,128)(2,1)}), bf16[32,8,2048]{2,1,0:T(8,128)(2,1)S(1)}, u32[]{:S(2)}, u32[]{:S(2)}) async-start(bf16[32,8,2048]{2,1,0:T(8,128)(2,1)} %broadcast_in_dim.4), calls=%async_computation | async-start | bytes 2097152 | tf_op jit(solution)/shard_map/all_to_all | solution.py:22
  67.2 1.4 copy-start.4
  68.7 19.5 %all-to-all-start.3 = ((bf16[16,16,512]{2,1,0:T(8,128)(2,1)}), bf16[16,16,512]{2,1,0:T(8,128)(2,1)S(1)}, u32[]{:S(2)}, u32[]{:S(2)}) async-start(bf16[16,16,512]{2,1,0:T(8,128)(2,1)} %bitcast.17), calls=%async_computation.3 | async-start | bytes 524288 | tf_op jit(solution)/shard_map/all_to_all | solution.py:52
  77.5 19.5 %copy-start.2 = (s32[16,4]{0,1:T(4,128)S(1)}, s32[16,4]{0,1:T(4,128)}, u32[]{:S(2)}) copy-start(s32[16,4]{0,1:T(4,128)} %param.7) | copy-start | bytes 772
  77.5 121.1 %copy-start.1 = (f32[16,512]{1,0:T(8,128)S(1)}, f32[16,512]{1,0:T(8,128)}, u32[]{:S(2)}) copy-start(f32[16,512]{1,0:T(8,128)} %param.9) | copy-start | bytes 98308
  77.5 121.7 %copy-start = (f32[8,2048]{1,0:T(8,128)S(1)}, f32[8,2048]{1,0:T(8,128)}, u32[]{:S(2)}) copy-start(f32[8,2048]{1,0:T(8,128)} %param.8) | copy-start | bytes 196612
  88.2 25.9 %all-to-all-start.2 = ((bf16[32,8,2048]{2,1,0:T(8,128)(2,1)}), bf16[32,8,2048]{2,1,0:T(8,128)(2,1)S(1)}, u32[]{:S(2)}, u32[]{:S(2)}) async-start(bf16[32,8,2048]{2,1,0:T(8,128)(2,1)} %fusion), calls=%async_computation.2 | async-start | bytes 2097152 | tf_op jit(solution)/shard_map/all_to_all | solution.py:52
